TPU v7x, 512 devices: a whole 4x8x8 slice. The times are simulated.
512 devices in a mesh: group: 2 (over core), dp: 64 (over y, x, z_hi), mp: 4 (over z_lo).
Axes of the slice: x: 4, y: 8, z: 8 (z_hi: 2, z_lo: 4; z = z_hi * 4 + z_lo), core: 2. Of those that a mesh axis runs over, the one named last changes fastest.
Arguments:
- x_arrive: bfloat16 [256, 256, 1152], P(('group', 'dp')), may hold values from -6 to 6
- cond_first: int32 [128], P(('group', 'dp')), may hold values 0 or 1
- labels: int32 [128], P(('group', 'dp')), may hold values from 0 to 999
- step_ids: int32 [128], P(('group', 'dp')), may hold values from 0 to 999
- guidance: float32 [1], replicated, may hold values from 2 to 6
- time_table: bfloat16 [1000, 1152], P(None, 'mp'), may hold values from -6 to 6
- class_table: bfloat16 [1001, 1152], P(None, 'mp'), may hold values from -6 to 6
- ada_weight: bfloat16 [1152, 6912], P('mp', 'dp'), may hold values from -0.1875 to 0.1875
- final_ada: bfloat16 [1152, 2304], P('mp'), may hold values from -0.1875 to 0.1875
- qkv_weight: bfloat16 [3, 1152, 1152], P(None, 'dp', 'mp'), may hold values from -2 to 2
- proj_weight: bfloat16 [1152, 1152], P('mp', 'dp'), may hold values from -0.1875 to 0.1875
- fc1_weight: bfloat16 [1152, 4608], P('dp', 'mp'), may hold values from -0.1875 to 0.1875
- fc2_weight: bfloat16 [4608, 1152], P('mp', 'dp'), may hold values from -0.09375 to 0.09375
- out_weight: bfloat16 [1152, 16], replicated, may hold values from -0.1875 to 0.1875
Outputs:
- guided: float32 [128, 4096], P(('group', 'dp'), 'mp')
All inputs are finite; a program needn't handle non-finite values. No bound on the sum of `cond_first` on one device may be relied on, other than what follows from the above.
Results may differ from a plain program's by a relative error of at most 0.025.
Values may be sent and summed in bfloat16 or wider, within the bound.
No kernel may reach another device: no remote copies, remote signals or barrier semaphores. Data moves between devices by JAX's collectives and lax.ppermute only.
A program may use at most 64 MiB of HBM per device.

v0:
```python
import jax
import jax.numpy as jnp
from jax import lax
from jax.sharding import Mesh
from jax.sharding import PartitionSpec as P

HEADS = 16
CLASSES = 1000
DP = ("dp_0", "dp_1", "dp_2")
GROUP_DP = ("group", "dp_0", "dp_1", "dp_2")


def from_everyone(x, axis):
    size = lax.axis_size(axis)
    return lax.all_to_all(jnp.broadcast_to(x[None], (size, *x.shape)), axis, 0, 0, tiled=True)


def laid_out(pieces, dim):
    pieces = jnp.moveaxis(pieces, 0, dim)
    shape = pieces.shape
    return pieces.reshape(*shape[:dim], shape[dim] * shape[dim + 1], *shape[dim + 2 :])


def collect(x, axis, dim):
    pieces = from_everyone(x, axis)
    return laid_out(pieces, dim)


def of_everyone(x, axis):
    everything = from_everyone(x, axis)
    return jnp.sum(everything.astype(jnp.float32), axis=0)


def gathered_by_axis(x, axes, dim):
    for axis in reversed(axes):
        x = lax.all_gather(x, axis, axis=dim, tiled=True)
    return x


def cut_along(x, dim, size):
    shape = x.shape
    pieces = x.reshape(*shape[:dim], size, shape[dim] // size, *shape[dim + 1 :])
    return jnp.moveaxis(pieces, dim, 0)


def sum_at_owner(x, axis, dim):
    size = lax.axis_size(axis)
    pieces = lax.all_to_all(cut_along(x, dim, size), axis, 0, 0, tiled=True)
    return jnp.sum(pieces.astype(jnp.float32), axis=0)


def layer_norm(values):
    mean = jnp.mean(values, axis=-1, keepdims=True)
    centred = values - mean
    spread = jnp.mean(centred * centred, axis=-1, keepdims=True)
    return centred * lax.rsqrt(spread + 1e-06)


def on_device(
    x_arrive,
    cond_first,
    labels,
    step_ids,
    guidance,
    time_table,
    class_table,
    ada_weight,
    final_ada,
    qkv_weight,
    proj_weight,
    fc1_weight,
    fc2_weight,
    out_weight,
):
    pair_count = labels.shape[0]
    tokens = x_arrive.shape[1]
    width = x_arrive.shape[2]
    image_count = 2 * pair_count
    row_count = image_count * tokens
    split_rows = x_arrive.reshape(pair_count, 2, tokens, width)
    first = (cond_first == 1)[:, None, None]
    cond_rows = jnp.where(first, split_rows[:, 0], split_rows[:, 1])
    uncond_rows = jnp.where(first, split_rows[:, 1], split_rows[:, 0])
    x_sides = jnp.stack([cond_rows, uncond_rows])
    time_part = jnp.take(time_table, step_ids, axis=0).astype(jnp.float32)
    class_part = jnp.take(class_table, labels, axis=0).astype(jnp.float32)
    null_part = class_table[CLASSES].astype(jnp.float32)[None, :]
    emb_sides = time_part[None] + jnp.stack([class_part, null_part])
    act_sides = jax.nn.silu(emb_sides).astype(jnp.bfloat16)
    images, acts = (x_sides, act_sides)
    images = images.reshape(image_count, tokens, width)
    acts = acts.reshape(image_count, act_sides.shape[2])
    partial_final = jnp.dot(acts, final_ada, preferred_element_type=jnp.float32)
    every_act = collect(acts, DP, 0)
    column_part = jnp.dot(every_act, ada_weight, preferred_element_type=jnp.float32)
    summed, fmods = (
        of_everyone(column_part.astype(jnp.bfloat16), "mp").astype(jnp.float32),
        of_everyone(partial_final.astype(jnp.bfloat16), "mp").astype(jnp.float32),
    )
    mods = lax.all_to_all(
        summed.astype(jnp.bfloat16), DP, split_axis=0, concat_axis=1, tiled=True
    ).astype(summed.dtype)
    shift_a, scale_a, gate_a, shift_m, scale_m, gate_m = jnp.split(mods, 6, axis=1)
    shift_f, scale_f = jnp.split(fmods, 2, axis=1)
    images_f = images.astype(jnp.float32)
    hidden = (layer_norm(images_f) * (1.0 + scale_a[:, None]) + shift_a[:, None]).astype(
        jnp.bfloat16
    )
    hidden = hidden.reshape(row_count, width)
    quarter = qkv_weight.shape[2]
    head_dim = width // HEADS
    local_heads = quarter // head_dim
    columns = hidden
    qkv = jnp.einsum(
        "rd,kdc->krc",
        columns,
        lax.all_gather(qkv_weight, DP, axis=1, tiled=True),
        preferred_element_type=jnp.float32,
    ).astype(jnp.bfloat16)
    query = qkv[0].reshape(image_count, tokens, local_heads, head_dim)
    keys = qkv[1].reshape(image_count, tokens, local_heads, head_dim)
    values = qkv[2].reshape(image_count, tokens, local_heads, head_dim)
    scores = jnp.einsum(
        "bqhe,bkhe->bhqk", query, keys, preferred_element_type=jnp.float32
    ) * head_dim ** (-0.5)
    probs = jax.nn.softmax(scores, axis=-1).astype(jnp.bfloat16)
    mixed = jnp.einsum("bhqk,bkhe->bqhe", probs, values, preferred_element_type=jnp.float32).astype(
        jnp.bfloat16
    )
    mixed = mixed.reshape(row_count, quarter)
    attn_part = jnp.dot(mixed, collect(proj_weight, DP, 1), preferred_element_type=jnp.float32)
    attn = (
        lax.psum(attn_part.astype(jnp.bfloat16), "mp")
        .astype(jnp.float32)
        .reshape(image_count, tokens, width)
    )
    first_sum = images_f + gate_a[:, None] * attn
    hidden_two = (layer_norm(first_sum) * (1.0 + scale_m[:, None]) + shift_m[:, None]).astype(
        jnp.bfloat16
    )
    hidden_two = hidden_two.reshape(row_count, width)
    ff_quarter = fc1_weight.shape[1]
    columns = hidden_two
    up = jnp.dot(columns, gathered_by_axis(fc1_weight, DP, 0), preferred_element_type=jnp.float32)
    gelu_h = (
        jax.nn.gelu(up, approximate=True)
        .astype(jnp.bfloat16)
        .reshape(image_count, tokens, ff_quarter)
    )
    down_full = gathered_by_axis(fc2_weight, DP, 1)
    token_share = tokens // lax.axis_size("mp")
    mlp = sum_at_owner(
        jnp.einsum("btf,fd->tbd", gelu_h, down_full, preferred_element_type=jnp.float32).astype(
            jnp.bfloat16
        ),
        "mp",
        0,
    )
    token_start = lax.axis_index("mp") * token_share
    own_first = lax.dynamic_slice_in_dim(first_sum, token_start, token_share, 1).transpose(1, 0, 2)
    second_sum = own_first + gate_m[None] * mlp
    fin = (layer_norm(second_sum) * (1.0 + scale_f[None]) + shift_f[None]).astype(jnp.bfloat16)
    noise = jnp.einsum("tbd,do->bto", fin, out_weight, preferred_element_type=jnp.float32)
    noise = noise.reshape(2, pair_count, token_share * out_weight.shape[1])
    return noise[1] + guidance[0] * (noise[0] - noise[1])


def solution(mesh):
    torus = Mesh(
        mesh.devices.reshape(mesh.shape["group"], 8, 4, 2, mesh.shape["mp"]),
        ("group", "dp_0", "dp_1", "dp_2", "mp"),
    )
    placed = (
        P(GROUP_DP, None, None),
        P(GROUP_DP),
        P(GROUP_DP),
        P(GROUP_DP),
        P(),
        P(None, "mp"),
        P(None, "mp"),
        P("mp", DP),
        P("mp", None),
        P(None, DP, "mp"),
        P("mp", DP),
        P(DP, "mp"),
        P("mp", DP),
        P(),
    )
    return jax.shard_map(
        on_device, mesh=torus, in_specs=placed, out_specs=P(GROUP_DP, "mp"), check_vma=False
    )
```

profile of v0, /device:TPU:4, one launch (start us, length us, event | category | flops | bytes accessed | tf_op | source)
XLA Modules:
  0.0 341.8 jit_solution(6708045404015547400)
XLA Ops:
  7.4 1.6 copy.106
  10.3 1.0 constant_dynamic-slice_fusion
  11.3 0.1 copy.119
  11.4 1.0 constant_dynamic-slice_fusion.1
  12.4 0.1 copy.118
  12.5 0.1 copy.120
  12.7 0.6 copy-done.6
  13.2 0.7 broadcast_in_dim.50
  13.9 19.2 %all-to-all-start = ((bf16[64,2,288]{2,1,0:T(2,128)(2,1)}), bf16[64,2,288]{2,1,0:T(2,128)(2,1)S(1)}, u32[]{:S(2)}, u32[]{:S(2)}) async-start(bf16[64,2,288]{2,1,0:T(2,128)(2,1)} %broadcast_in_dim.50), calls=%async_computation | async-start | bytes 196608 | tf_op jit(solution)/shard_map/all_to_all | solution.py:15
  33.8 12.4 %all-to-all-done = bf16[64,2,288]{2,1,0:T(2,128)(2,1)S(1)} async-done(((bf16[64,2,288]{2,1,0:T(2,128)(2,1)}), bf16[64,2,288]{2,1,0:T(2,128)(2,1)S(1)}, u32[]{:S(2)}, u32[]{:S(2)}) %all-to-all-start) | async-done | bytes 73760 | tf_op jit(solution)/shard_map/all_to_all | solution.py:15
  46.3 1.1 convolution_convert_fusion.4
  47.4 0.7 broadcast_in_dim.84
  48.1 4.5 %all-to-all-start.1 = ((bf16[4,128,108]{1,2,0:T(8,128)(2,1)}), bf16[4,128,108]{1,2,0:T(8,128)(2,1)S(1)}, u32[]{:S(2)}, u32[]{:S(2)}) async-start(bf16[4,128,108]{1,2,0:T(8,128)(2,1)} %broadcast_in_dim.84), calls=%async_computation.1 | async-start | bytes 229376 | tf_op jit(solution)/shard_map/all_to_all | solution.py:15
  52.6 1.4 broadcast_select_fusion.1
  53.9 4.5 %all-to-all-done.1 = bf16[4,128,108]{1,2,0:T(8,128)(2,1)S(1)} async-done(((bf16[4,128,108]{1,2,0:T(8,128)(2,1)}), bf16[4,128,108]{1,2,0:T(8,128)(2,1)S(1)}, u32[]{:S(2)}, u32[]{:S(2)}) %all-to-all-start.1) | async-done | bytes 110624 | tf_op jit(solution)/shard_map/all_to_all | solution.py:15
  58.5 0.7 copy.104
  59.2 6.2 %all-to-all-start.2 = ((bf16[64,2,108]{2,1,0:T(2,128)(2,1)}), bf16[64,2,108]{2,1,0:T(2,128)(2,1)S(1)}, u32[]{:S(2)}, u32[]{:S(2)}) async-start(bf16[64,2,108]{2,1,0:T(2,128)(2,1)} %bitcast.7), calls=%async_computation.2 | async-start | bytes 65536 | tf_op jit(solution)/shard_map/all_to_all | solution.py:100
  65.3 0.2 convert_reduce_fusion
  65.6 12.4 %all-to-all-done.2 = bf16[64,2,108]{2,1,0:T(2,128)(2,1)S(1)} async-done(((bf16[64,2,108]{2,1,0:T(2,128)(2,1)}), bf16[64,2,108]{2,1,0:T(2,128)(2,1)S(1)}, u32[]{:S(2)}, u32[]{:S(2)}) %all-to-all-start.2) | async-done | bytes 27680 | tf_op jit(solution)/shard_map/all_to_all | solution.py:100
  78.0 1.1 broadcast_in_dim.85
  79.1 7.2 %all-to-all-start.3 = ((bf16[64,288,18]{1,2,0:T(8,128)(2,1)}), bf16[64,288,18]{1,2,0:T(8,128)(2,1)}, u32[]{:S(2)}, u32[]{:S(2)}) async-start(bf16[64,288,18]{1,2,0:T(8,128)(2,1)} %broadcast_in_dim.85), calls=%async_computation.3 | async-start | bytes 2359296 | tf_op jit(solution)/shard_map/all_to_all | solution.py:15
  86.4 0.4 fusion.20
  86.9 0.1 reshape.305
  87.1 1.7 fusion.16
  88.8 30.6 %all-to-all-done.3 = bf16[64,288,18]{1,2,0:T(8,128)(2,1)} async-done(((bf16[64,288,18]{1,2,0:T(8,128)(2,1)}), bf16[64,288,18]{1,2,0:T(8,128)(2,1)}, u32[]{:S(2)}, u32[]{:S(2)}) %all-to-all-start.3) | async-done | bytes 663584 | tf_op jit(solution)/shard_map/all_to_all | solution.py:15
  119.4 1.6 reshape.262
  121.0 51.8 %all-gather.8.cloned.1.call-done = bf16[3,1152,288]{2,0,1:T(4,128)(2,1)} async-done(((bf16[3,18,288]{2,0,1:T(4,128)(2,1)}), bf16[3,1152,288]{2,0,1:T(4,128)(2,1)}) %all-gather.8.cloned.1.call-update) | async-done | bytes 1990672 | tf_op jit(solution)/shard_map/all_gather | solution.py:117
  172.8 3.7 %fusion.26 = bf16[3,512,288]{1,2,0:T(8,128)(2,1)S(1)} fusion(bf16[3,1152,288]{2,0,1:T(4,128)(2,1)} %all-gather.8.cloned.1.call-done, bf16[512,1152]{1,0:T(8,128)(2,1)} %fusion.16), kind=kOutput, calls=%fused_computation.41 | convolution fusion | flops 1019658240 | bytes 4055040 | tf_op jit(solution)/shard_map/rd,kdc->krc/dot_general | solution.py:114
  176.6 0.9 fusion.62
  177.5 1.7 reshape_squeeze.10
  179.3 1.7 reshape_squeeze.11
  181.0 1.8 reshape_squeeze.9
  182.8 3.2 fusion.65
  186.0 2.0 fusion.30
  188.0 0.3 copy.112
  188.4 2.0 convolution_convert_fusion.2
  190.4 9.3 %all-gather = bf16[2,18,1152]{2,1,0:T(8,128)(2,1)S(1)} all-gather(bf16[1,18,1152]{2,1,0:T(8,128)(2,1)S(1)} %bitcast.125), channel_id=1, replica_groups=mesh['group'=2,'dp_0'=8,'dp_1'=4,'dp_2'=2,'mp'=4] {'dp_2'}, dimensions={0}, use_global_device_ids=true | all-gather | bytes 124416 | tf_op jit(solution)/shard_map/all_gather | solution.py:36
  199.8 11.3 %all-gather.1 = bf16[4,36,1152]{2,1,0:T(8,128)(2,1)S(1)} all-gather(bf16[1,36,1152]{2,1,0:T(8,128)(2,1)S(1)} %reshape.323), channel_id=1, replica_groups=mesh['group'=2,'dp_0'=8,'dp_1'=4,'dp_2'=2,'mp'=4] {'dp_1'}, dimensions={0}, use_global_device_ids=true | all-gather | bytes 414720 | tf_op jit(solution)/shard_map/all_gather | solution.py:36
  211.0 0.8 reshape.324
  211.9 10.3 %all-gather.2 = bf16[2,18,1152]{2,1,0:T(8,128)(2,1)S(1)} all-gather(bf16[1,18,1152]{2,1,0:T(8,128)(2,1)S(1)} %bitcast.126), channel_id=1, replica_groups=mesh['group'=2,'dp_0'=8,'dp_1'=4,'dp_2'=2,'mp'=4] {'dp_2'}, dimensions={0}, use_global_device_ids=true | all-gather | bytes 124416 | tf_op jit(solution)/shard_map/all_gather | solution.py:36
  222.2 12.4 %all-gather.3 = bf16[4,36,1152]{2,1,0:T(8,128)(2,1)S(1)} all-gather(bf16[1,36,1152]{2,1,0:T(8,128)(2,1)S(1)} %reshape.327), channel_id=1, replica_groups=mesh['group'=2,'dp_0'=8,'dp_1'=4,'dp_2'=2,'mp'=4] {'dp_1'}, dimensions={0}, use_global_device_ids=true | all-gather | bytes 414720 | tf_op jit(solution)/shard_map/all_gather | solution.py:36
  234.7 0.8 reshape.328
  235.6 0.3 convolution_convert_fusion
  235.9 0.6 broadcast_in_dim.86
  236.5 3.4 %all-to-all-start.5 = ((bf16[4,2,2304]{2,1,0:T(2,128)(2,1)}), bf16[4,2,2304]{2,1,0:T(2,128)(2,1)S(1)}, u32[]{:S(2)}, u32[]{:S(2)}) async-start(bf16[4,2,2304]{2,1,0:T(2,128)(2,1)} %broadcast_in_dim.86), calls=%async_computation.5 | async-start | bytes 73728 | tf_op jit(solution)/shard_map/all_to_all | solution.py:15
  240.0 21.1 %all-reduce.2.cloned.1.call-done = bf16[512,1152]{1,0:T(8,128)(2,1)} async-done(((bf16[512,1152]{1,0:T(8,128)(2,1)}), bf16[512,1152]{1,0:T(8,128)(2,1)}) %all-reduce.2.cloned.1.call-update) | async-done | bytes 1179664 | tf_op jit(solution)/shard_map/psum | solution.py:133
  261.1 1.7 fusion.60
  262.8 1.4 copy-done.1
  264.2 0.4 multiply_reduce_fusion
  264.6 0.3 copy-done.2
  264.9 2.0 fusion.12
  266.9 4.0 %fusion.11 = bf16[512,1152]{1,0:T(8,128)(2,1)S(1)} fusion(bf16[512,1152]{1,0:T(8,128)(2,1)} %fusion.12, bf16[1152,1152]{1,0:T(8,128)(2,1)} %all-gather.10.cloned.1.call-done), kind=kOutput, calls=%fused_computation.15 | convolution fusion | flops 1364262912 | bytes 5013504 | tf_op jit(solution)/shard_map/dot_general | solution.py:144
  271.0 25.5 %all-gather.12.cloned.1.call-done = bf16[1152,1152]{0,1:T(8,128)(2,1)} async-done(((bf16[1152,144]{0,1:T(8,128)(2,1)}), bf16[1152,1152]{0,1:T(8,128)(2,1)}) %all-gather.12.cloned.1.call-update) | async-done | bytes 2654224 | tf_op jit(solution)/shard_map/all_gather | solution.py:36
  296.4 3.6 %convolution_convert_fusion.1 = bf16[2,256,1152]{2,1,0:T(8,128)(2,1)S(1)} fusion(bf16[2,256,1152]{2,1,0:T(8,128)(2,1)S(1)} %bitcast.131, bf16[1152,1152]{0,1:T(8,128)(2,1)} %all-gather.12.cloned.1.call-done), kind=kOutput, calls=%fused_computation.3 | convolution fusion | flops 1359544320 | bytes 5013504 | tf_op jit(solution)/shard_map/btf,fd->tbd/dot_general | solution.py:153
  300.0 1.1 copy.113
  301.2 4.8 %all-to-all-start.4 = ((bf16[4,64,2,1152]{3,1,2,0:T(8,128)(2,1)}), bf16[4,64,2,1152]{3,1,2,0:T(8,128)(2,1)S(1)}, u32[]{:S(2)}, u32[]{:S(2)}) async-start(bf16[4,64,2,1152]{3,1,2,0:T(8,128)(2,1)} %copy.113), calls=%async_computation.4 | async-start | bytes 2359296 | tf_op jit(solution)/shard_map/all_to_all | solution.py:48
  306.7 24.8 %all-to-all-done.4 = bf16[4,64,2,1152]{3,1,2,0:T(8,128)(2,1)S(1)} async-done(((bf16[4,64,2,1152]{3,1,2,0:T(8,128)(2,1)}), bf16[4,64,2,1152]{3,1,2,0:T(8,128)(2,1)S(1)}, u32[]{:S(2)}, u32[]{:S(2)}) %all-to-all-start.4) | async-done | bytes 1179680 | tf_op jit(solution)/shard_map/all_to_all | solution.py:48
  331.5 0.2 convert_reduce_fusion.1
  331.6 1.2 fusion.59
  332.8 0.2 multiply_reduce_fusion.2
  333.1 0.3 convolution_bitcast_fusion
  333.4 0.1 copy.115
  333.5 0.1 squeeze.6
  333.8 0.6 multiply_add_fusion
  (51 shorter events, 0.8 us)
Async XLA Ops:
  7.4 228.2 %copy-start = (bf16[288,2304]{1,0:T(8,128)(2,1)S(1)}, bf16[288,2304]{1,0:T(8,128)(2,1)}, u32[]{:S(2)}) copy-start(bf16[288,2304]{1,0:T(8,128)(2,1)} %param.22) | copy-start | bytes 3981316
  7.4 165.5 %all-gather.8.cloned.1.call-start = ((), (), s32[]{:S(2)}) async-start(), calls=%async_computation.6 | async-start | bytes 3594240 | tf_op jit(solution)/shard_map/all_gather | solution.py:117
  12.7 0.6 copy-start.6
  13.9 64.1 %copy-start.5 = (bf16[288,18]{0,1:T(8,128)(2,1)S(1)}, bf16[288,18]{0,1:T(8,128)(2,1)}, u32[]{:S(2)}) copy-start(bf16[288,18]{0,1:T(8,128)(2,1)} %param.24) | copy-start | bytes 31108
  13.9 32.3 %all-to-all-start = ((bf16[64,2,288]{2,1,0:T(2,128)(2,1)}), bf16[64,2,288]{2,1,0:T(2,128)(2,1)S(1)}, u32[]{:S(2)}, u32[]{:S(2)}) async-start(bf16[64,2,288]{2,1,0:T(2,128)(2,1)} %broadcast_in_dim.50), calls=%async_computation | async-start | bytes 196608 | tf_op jit(solution)/shard_map/all_to_all | solution.py:15
  48.1 10.4 %all-to-all-start.1 = ((bf16[4,128,108]{1,2,0:T(8,128)(2,1)}), bf16[4,128,108]{1,2,0:T(8,128)(2,1)S(1)}, u32[]{:S(2)}, u32[]{:S(2)}) async-start(bf16[4,128,108]{1,2,0:T(8,128)(2,1)} %broadcast_in_dim.84), calls=%async_computation.1 | async-start | bytes 229376 | tf_op jit(solution)/shard_map/all_to_all | solution.py:15
  59.2 18.8 %all-to-all-start.2 = ((bf16[64,2,108]{2,1,0:T(2,128)(2,1)}), bf16[64,2,108]{2,1,0:T(2,128)(2,1)S(1)}, u32[]{:S(2)}, u32[]{:S(2)}) async-start(bf16[64,2,108]{2,1,0:T(2,128)(2,1)} %bitcast.7), calls=%async_computation.2 | async-start | bytes 65536 | tf_op jit(solution)/shard_map/all_to_all | solution.py:100
  79.1 40.3 %all-to-all-start.3 = ((bf16[64,288,18]{1,2,0:T(8,128)(2,1)}), bf16[64,288,18]{1,2,0:T(8,128)(2,1)}, u32[]{:S(2)}, u32[]{:S(2)}) async-start(bf16[64,288,18]{1,2,0:T(8,128)(2,1)} %broadcast_in_dim.85), calls=%async_computation.3 | async-start | bytes 2359296 | tf_op jit(solution)/shard_map/all_to_all | solution.py:15
  86.3 174.8 %all-reduce.2.cloned.1.call-start = ((), (), s32[]{:S(2)}) async-start(), calls=%async_computation.7 | async-start | bytes 2359296 | tf_op jit(solution)/shard_map/psum | solution.py:133
  188.0 2.4 copy-start.3
  188.4 23.6 %copy-start.4 = (bf16[1152,18]{0,1:T(8,128)(2,1)S(1)}, bf16[1152,18]{0,1:T(8,128)(2,1)}, u32[]{:S(2)}) copy-start(bf16[1152,18]{0,1:T(8,128)(2,1)} %param.26) | copy-start | bytes 124420
  190.3 45.2 %copy-start.7 = (bf16[2,288]{1,0:T(2,128)(2,1)S(1)}, bf16[2,288]{1,0:T(2,128)(2,1)}, u32[]{:S(2)}) copy-start(bf16[2,288]{1,0:T(2,128)(2,1)} %copy-done.6) | copy-start | bytes 3460
  190.4 76.6 %all-gather.10.cloned.1.call-start = ((), (), s32[]{:S(2)}) async-start(), calls=%async_computation.8 | async-start | bytes 2985984 | tf_op jit(solution)/shard_map/all_gather | solution.py:36
  211.9 84.6 %all-gather.12.cloned.1.call-start = ((), (), s32[]{:S(2)}) async-start(), calls=%async_computation.9 | async-start | bytes 2985984 | tf_op jit(solution)/shard_map/all_gather | solution.py:36
  236.5 64.7 %all-to-all-start.5 = ((bf16[4,2,2304]{2,1,0:T(2,128)(2,1)}), bf16[4,2,2304]{2,1,0:T(2,128)(2,1)S(1)}, u32[]{:S(2)}, u32[]{:S(2)}) async-start(bf16[4,2,2304]{2,1,0:T(2,128)(2,1)} %broadcast_in_dim.86), calls=%async_computation.5 | async-start | bytes 73728 | tf_op jit(solution)/shard_map/all_to_all | solution.py:15
  262.8 1.4 copy-start.1
  262.8 2.1 copy-start.2
  301.2 30.3 %all-to-all-start.4 = ((bf16[4,64,2,1152]{3,1,2,0:T(8,128)(2,1)}), bf16[4,64,2,1152]{3,1,2,0:T(8,128)(2,1)S(1)}, u32[]{:S(2)}, u32[]{:S(2)}) async-start(bf16[4,64,2,1152]{3,1,2,0:T(8,128)(2,1)} %copy.113), calls=%async_computation.4 | async-start | bytes 2359296 | tf_op jit(solution)/shard_map/all_to_all | solution.py:48
  305.9 27.1 %copy-start.8 = (bf16[1152,16]{0,1:T(8,128)(2,1)S(1)}, bf16[1152,16]{0,1:T(8,128)(2,1)}, u32[]{:S(2)}) copy-start(bf16[1152,16]{0,1:T(8,128)(2,1)} %param.27) | copy-start | bytes 110596
Sparse Core Ops, SparseCore 0:
  12.5 160.2 all-gather.7
  190.5 70.5 all-reduce.1
Sparse Core Ops, SparseCore 1:
  212.0 38.8 all-gather.9
  252.8 43.6 all-gather.11
where the time goes:
time: 343 us; the launch traced here: 342 us
  waiting for transfers between devices  183 us (53%)
  starting transfers between devices  45.4 us (13%)
  blocking collectives  43.3 us (13%)
  local copies, waits for them, and re-layouts  21.6 us (6%)
  matrix products  20.2 us (6%)
  between operations  17.8 us (5%)
  other arithmetic  10.3 us (3%)
    all_gather x1, waiting for transfers between devices, on_device(): lax.all_gather(qkv_weight, DP, axis=1, tiled=True)  51.8 us
    all_to_all x4, waiting for transfers between devices, from_everyone(): lax.all_to_all(jnp.broadcast_to(x[None], (size, *x.shape)), axis, 0, 0, t...  47.6 us
    all_gather x4, blocking collectives, gathered_by_axis(): x = lax.all_gather(x, axis, axis=dim, tiled=True)  43.3 us
    all_to_all x4, starting transfers between devices, from_everyone(): lax.all_to_all(jnp.broadcast_to(x[None], (size, *x.shape)), axis, 0, 0, t...  34.3 us
    all_gather x2, waiting for transfers between devices, gathered_by_axis(): x = lax.all_gather(x, axis, axis=dim, tiled=True)  25.5 us
    all_to_all x1, waiting for transfers between devices, sum_at_owner(): pieces = lax.all_to_all(cut_along(x, dim, size), axis, 0, 0, tiled=True)  24.8 us
    psum x1, waiting for transfers between devices, on_device(): lax.psum(attn_part.astype(jnp.bfloat16), 'mp').astype(jnp.float32)  21.1 us
    all_to_all x1, waiting for transfers between devices, on_device(): lax.all_to_all(summed.astype(jnp.bfloat16), DP, split_axis=0, concat_axis...  12.4 us
  transfers between devices with their start and end apart: 10, of which 8 were waited for; matrix products, arithmetic and copies ran while one was open for 8% of the time, Pallas kernels for 0%

commit v1 on v0

--- a/solution.py
+++ b/solution.py
@@ -8,6 +8,11 @@
 CLASSES = 1000
 DP = ("dp_0", "dp_1", "dp_2")
 GROUP_DP = ("group", "dp_0", "dp_1", "dp_2")
+
+
+def summed_here(value, name):
+    terms = lax.all_gather(value, name)
+    return jnp.sum(terms, axis=0)
 
 
 def from_everyone(x, axis):
@@ -130,7 +135,7 @@
     mixed = mixed.reshape(row_count, quarter)
     attn_part = jnp.dot(mixed, collect(proj_weight, DP, 1), preferred_element_type=jnp.float32)
     attn = (
-        lax.psum(attn_part.astype(jnp.bfloat16), "mp")
+        summed_here(attn_part.astype(jnp.bfloat16), "mp")
         .astype(jnp.float32)
         .reshape(image_count, tokens, width)
     )

time: 343 us -> 420 us (1.22)
  the two profiles are of different devices: /device:TPU:4 before, /device:TPU:2 now
where the time goes in v1:
time: 420 us; the launch traced here: 419 us
  waiting for transfers between devices  257 us (61%)
  blocking collectives  44.9 us (11%)
  starting transfers between devices  44.3 us (11%)
  local copies, waits for them, and re-layouts  21.6 us (5%)
  matrix products  20.1 us (5%)
  between operations  16.1 us (4%)
  other arithmetic  14.5 us (3%)
    all_gather x2, waiting for transfers between devices, gathered_by_axis(): x = lax.all_gather(x, axis, axis=dim, tiled=True)  78.3 us
    all_gather x1, waiting for transfers between devices, on_device(): lax.all_gather(qkv_weight, DP, axis=1, tiled=True)  51.7 us
    all_to_all x4, waiting for transfers between devices, from_everyone(): lax.all_to_all(jnp.broadcast_to(x[None], (size, *x.shape)), axis, 0, 0, t...  48.5 us
    all_gather x4, blocking collectives, gathered_by_axis(): x = lax.all_gather(x, axis, axis=dim, tiled=True)  44.9 us
    all_gather x1, waiting for transfers between devices, summed_here(): terms = lax.all_gather(value, name)  41 us
    all_to_all x4, starting transfers between devices, from_everyone(): lax.all_to_all(jnp.broadcast_to(x[None], (size, *x.shape)), axis, 0, 0, t...  33.8 us
    all_to_all x1, waiting for transfers between devices, sum_at_owner(): pieces = lax.all_to_all(cut_along(x, dim, size), axis, 0, 0, tiled=True)  24.7 us
    all_to_all x1, waiting for transfers between devices, on_device(): lax.all_to_all(summed.astype(jnp.bfloat16), DP, split_axis=0, concat_axis...  13.3 us
  transfers between devices with their start and end apart: 10, of which 9 were waited for; matrix products, arithmetic and copies ran while one was open for 8% of the time, Pallas kernels for 0%

profile of v1, /device:TPU:2, one launch (start us, length us, event | category | flops | bytes accessed | tf_op | source)
XLA Modules:
  0.0 419.0 jit_solution(1821897589732077822)
XLA Ops:
  6.5 1.6 copy.106
  9.4 1.0 constant_dynamic-slice_fusion
  10.6 1.0 constant_dynamic-slice_fusion.1
  11.6 0.1 copy.120
  11.9 0.6 copy-done.6
  12.4 0.7 broadcast_in_dim.50
  13.1 19.2 %all-to-all-start = ((bf16[64,2,288]{2,1,0:T(2,128)(2,1)}), bf16[64,2,288]{2,1,0:T(2,128)(2,1)S(1)}, u32[]{:S(2)}, u32[]{:S(2)}) async-start(bf16[64,2,288]{2,1,0:T(2,128)(2,1)} %broadcast_in_dim.50), calls=%async_computation | async-start | bytes 196608 | tf_op jit(solution)/shard_map/all_to_all | solution.py:20
  33.0 13.1 %all-to-all-done = bf16[64,2,288]{2,1,0:T(2,128)(2,1)S(1)} async-done(((bf16[64,2,288]{2,1,0:T(2,128)(2,1)}), bf16[64,2,288]{2,1,0:T(2,128)(2,1)S(1)}, u32[]{:S(2)}, u32[]{:S(2)}) %all-to-all-start) | async-done | bytes 73760 | tf_op jit(solution)/shard_map/all_to_all | solution.py:20
  46.2 1.1 convolution_convert_fusion.4
  47.3 0.7 broadcast_in_dim.84
  48.0 4.6 %all-to-all-start.1 = ((bf16[4,128,108]{1,2,0:T(8,128)(2,1)}), bf16[4,128,108]{1,2,0:T(8,128)(2,1)S(1)}, u32[]{:S(2)}, u32[]{:S(2)}) async-start(bf16[4,128,108]{1,2,0:T(8,128)(2,1)} %broadcast_in_dim.84), calls=%async_computation.1 | async-start | bytes 229376 | tf_op jit(solution)/shard_map/all_to_all | solution.py:20
  52.5 1.4 broadcast_select_fusion.1
  53.9 4.5 %all-to-all-done.1 = bf16[4,128,108]{1,2,0:T(8,128)(2,1)S(1)} async-done(((bf16[4,128,108]{1,2,0:T(8,128)(2,1)}), bf16[4,128,108]{1,2,0:T(8,128)(2,1)S(1)}, u32[]{:S(2)}, u32[]{:S(2)}) %all-to-all-start.1) | async-done | bytes 110624 | tf_op jit(solution)/shard_map/all_to_all | solution.py:20
  58.4 0.7 copy.104
  59.1 5.4 %all-to-all-start.2 = ((bf16[64,2,108]{2,1,0:T(2,128)(2,1)}), bf16[64,2,108]{2,1,0:T(2,128)(2,1)S(1)}, u32[]{:S(2)}, u32[]{:S(2)}) async-start(bf16[64,2,108]{2,1,0:T(2,128)(2,1)} %bitcast.7), calls=%async_computation.2 | async-start | bytes 65536 | tf_op jit(solution)/shard_map/all_to_all | solution.py:105
  64.5 0.2 convert_reduce_fusion
  64.7 13.3 %all-to-all-done.2 = bf16[64,2,108]{2,1,0:T(2,128)(2,1)S(1)} async-done(((bf16[64,2,108]{2,1,0:T(2,128)(2,1)}), bf16[64,2,108]{2,1,0:T(2,128)(2,1)S(1)}, u32[]{:S(2)}, u32[]{:S(2)}) %all-to-all-start.2) | async-done | bytes 27680 | tf_op jit(solution)/shard_map/all_to_all | solution.py:105
  78.0 1.1 broadcast_in_dim.85
  79.1 6.3 %all-to-all-start.3 = ((bf16[64,288,18]{1,2,0:T(8,128)(2,1)}), bf16[64,288,18]{1,2,0:T(8,128)(2,1)}, u32[]{:S(2)}, u32[]{:S(2)}) async-start(bf16[64,288,18]{1,2,0:T(8,128)(2,1)} %broadcast_in_dim.85), calls=%async_computation.3 | async-start | bytes 2359296 | tf_op jit(solution)/shard_map/all_to_all | solution.py:20
  85.5 0.4 fusion.20
  86.1 0.1 reshape.305
  86.2 1.7 fusion.16
  87.9 30.8 %all-to-all-done.3 = bf16[64,288,18]{1,2,0:T(8,128)(2,1)} async-done(((bf16[64,288,18]{1,2,0:T(8,128)(2,1)}), bf16[64,288,18]{1,2,0:T(8,128)(2,1)}, u32[]{:S(2)}, u32[]{:S(2)}) %all-to-all-start.3) | async-done | bytes 663584 | tf_op jit(solution)/shard_map/all_to_all | solution.py:20
  118.7 1.6 reshape.263
  120.4 51.7 %all-gather.10.cloned.1.call-done = bf16[3,1152,288]{2,0,1:T(4,128)(2,1)} async-done(((bf16[3,18,288]{2,0,1:T(4,128)(2,1)}), bf16[3,1152,288]{2,0,1:T(4,128)(2,1)}) %all-gather.10.cloned.1.call-update) | async-done | bytes 1990672 | tf_op jit(solution)/shard_map/all_gather | solution.py:122
  172.1 3.7 fusion.26
  175.8 0.9 fusion.62
  176.8 1.7 reshape_squeeze.10
  178.5 1.7 reshape_squeeze.11
  180.2 1.8 reshape_squeeze.9
  182.0 3.2 fusion.65
  185.2 2.0 fusion.30
  187.2 0.3 copy.112
  187.6 1.9 convolution_convert_fusion.2
  189.6 9.3 %all-gather.1 = bf16[2,18,1152]{2,1,0:T(8,128)(2,1)S(1)} all-gather(bf16[1,18,1152]{2,1,0:T(8,128)(2,1)S(1)} %bitcast.127), channel_id=1, replica_groups=mesh['group'=2,'dp_0'=8,'dp_1'=4,'dp_2'=2,'mp'=4] {'dp_2'}, dimensions={0}, use_global_device_ids=true | all-gather | bytes 124416 | tf_op jit(solution)/shard_map/all_gather | solution.py:41
  198.9 12.5 %all-gather.2 = bf16[4,36,1152]{2,1,0:T(8,128)(2,1)S(1)} all-gather(bf16[1,36,1152]{2,1,0:T(8,128)(2,1)S(1)} %reshape.325), channel_id=1, replica_groups=mesh['group'=2,'dp_0'=8,'dp_1'=4,'dp_2'=2,'mp'=4] {'dp_1'}, dimensions={0}, use_global_device_ids=true | all-gather | bytes 414720 | tf_op jit(solution)/shard_map/all_gather | solution.py:41
  211.4 0.8 reshape.326
  212.3 10.6 %all-gather.3 = bf16[2,18,1152]{2,1,0:T(8,128)(2,1)S(1)} all-gather(bf16[1,18,1152]{2,1,0:T(8,128)(2,1)S(1)} %bitcast.128), channel_id=1, replica_groups=mesh['group'=2,'dp_0'=8,'dp_1'=4,'dp_2'=2,'mp'=4] {'dp_2'}, dimensions={0}, use_global_device_ids=true | all-gather | bytes 124416 | tf_op jit(solution)/shard_map/all_gather | solution.py:41
  222.9 12.5 %all-gather.4 = bf16[4,36,1152]{2,1,0:T(8,128)(2,1)S(1)} all-gather(bf16[1,36,1152]{2,1,0:T(8,128)(2,1)S(1)} %reshape.329), channel_id=1, replica_groups=mesh['group'=2,'dp_0'=8,'dp_1'=4,'dp_2'=2,'mp'=4] {'dp_1'}, dimensions={0}, use_global_device_ids=true | all-gather | bytes 414720 | tf_op jit(solution)/shard_map/all_gather | solution.py:41
  235.4 0.8 reshape.330
  236.2 0.3 convolution_convert_fusion
  236.5 0.6 broadcast_in_dim.86
  237.2 3.6 all-to-all-start.5
  240.8 41.0 %all-gather.16.cloned.1.call-done = bf16[2048,1152]{1,0:T(8,128)(2,1)} async-done(((bf16[512,1152]{1,0:T(8,128)(2,1)}), bf16[2048,1152]{1,0:T(8,128)(2,1)}) %all-gather.16.cloned.1.call-update) | async-done | bytes 4718608 | tf_op jit(solution)/shard_map/all_gather | solution.py:14
  281.8 4.4 %reduce_sum.109 = bf16[512,1152]{1,0:T(8,128)(2,1)} reduce(bf16[4,512,1152]{2,1,0:T(8,128)(2,1)} %bitcast.121, bf16[]{:T(256)} %constant.37.clone.1), dimensions={0}, to_apply=%region_5.6 | reduce | flops 1769472 | bytes 5898242 | tf_op jit(solution)/shard_map/reduce_sum | solution.py:15
  286.2 1.7 fusion.60
  287.9 1.4 copy-done.1
  289.3 0.4 multiply_reduce_fusion
  289.7 0.3 copy-done.2
  290.0 1.9 fusion.12
  291.9 36.7 %all-gather.12.cloned.1.call-done = bf16[1152,1152]{1,0:T(8,128)(2,1)} async-done(((bf16[144,1152]{1,0:T(8,128)(2,1)}), bf16[1152,1152]{1,0:T(8,128)(2,1)}) %all-gather.12.cloned.1.call-update) | async-done | bytes 2654224 | tf_op jit(solution)/shard_map/all_gather | solution.py:41
  328.6 4.0 fusion.11
  332.6 41.6 %all-gather.14.cloned.1.call-done = bf16[1152,1152]{0,1:T(8,128)(2,1)} async-done(((bf16[1152,144]{0,1:T(8,128)(2,1)}), bf16[1152,1152]{0,1:T(8,128)(2,1)}) %all-gather.14.cloned.1.call-update) | async-done | bytes 2654224 | tf_op jit(solution)/shard_map/all_gather | solution.py:41
  374.2 3.6 convolution_convert_fusion.1
  377.8 1.1 copy.113
  379.0 5.1 %all-to-all-start.4 = ((bf16[4,64,2,1152]{3,1,2,0:T(8,128)(2,1)}), bf16[4,64,2,1152]{3,1,2,0:T(8,128)(2,1)S(1)}, u32[]{:S(2)}, u32[]{:S(2)}) async-start(bf16[4,64,2,1152]{3,1,2,0:T(8,128)(2,1)} %copy.113), calls=%async_computation.4 | async-start | bytes 2359296 | tf_op jit(solution)/shard_map/all_to_all | solution.py:53
  384.8 24.7 %all-to-all-done.4 = bf16[4,64,2,1152]{3,1,2,0:T(8,128)(2,1)S(1)} async-done(((bf16[4,64,2,1152]{3,1,2,0:T(8,128)(2,1)}), bf16[4,64,2,1152]{3,1,2,0:T(8,128)(2,1)S(1)}, u32[]{:S(2)}, u32[]{:S(2)}) %all-to-all-start.4) | async-done | bytes 1179680 | tf_op jit(solution)/shard_map/all_to_all | solution.py:53
  409.5 0.2 convert_reduce_fusion.1
  409.6 1.2 fusion.59
  410.9 0.2 multiply_reduce_fusion.2
  411.1 0.3 convolution_bitcast_fusion
  411.4 0.1 copy.115
  411.5 0.1 squeeze.6
  411.8 0.6 multiply_add_fusion
  (52 shorter events, 1.0 us)
Async XLA Ops:
  6.5 229.7 %copy-start = (bf16[288,2304]{1,0:T(8,128)(2,1)S(1)}, bf16[288,2304]{1,0:T(8,128)(2,1)}, u32[]{:S(2)}) copy-start(bf16[288,2304]{1,0:T(8,128)(2,1)} %param.22) | copy-start | bytes 3981316
  6.5 165.5 %all-gather.10.cloned.1.call-start = ((), (), s32[]{:S(2)}) async-start(), calls=%async_computation.6 | async-start | bytes 3594240 | tf_op jit(solution)/shard_map/all_gather | solution.py:122
  11.8 0.6 copy-start.6
  13.1 64.9 %copy-start.5 = (bf16[288,18]{0,1:T(8,128)(2,1)S(1)}, bf16[288,18]{0,1:T(8,128)(2,1)}, u32[]{:S(2)}) copy-start(bf16[288,18]{0,1:T(8,128)(2,1)} %param.24) | copy-start | bytes 31108
  13.1 33.0 %all-to-all-start = ((bf16[64,2,288]{2,1,0:T(2,128)(2,1)}), bf16[64,2,288]{2,1,0:T(2,128)(2,1)S(1)}, u32[]{:S(2)}, u32[]{:S(2)}) async-start(bf16[64,2,288]{2,1,0:T(2,128)(2,1)} %broadcast_in_dim.50), calls=%async_computation | async-start | bytes 196608 | tf_op jit(solution)/shard_map/all_to_all | solution.py:20
  48.0 10.4 %all-to-all-start.1 = ((bf16[4,128,108]{1,2,0:T(8,128)(2,1)}), bf16[4,128,108]{1,2,0:T(8,128)(2,1)S(1)}, u32[]{:S(2)}, u32[]{:S(2)}) async-start(bf16[4,128,108]{1,2,0:T(8,128)(2,1)} %broadcast_in_dim.84), calls=%async_computation.1 | async-start | bytes 229376 | tf_op jit(solution)/shard_map/all_to_all | solution.py:20
  59.1 18.9 %all-to-all-start.2 = ((bf16[64,2,108]{2,1,0:T(2,128)(2,1)}), bf16[64,2,108]{2,1,0:T(2,128)(2,1)S(1)}, u32[]{:S(2)}, u32[]{:S(2)}) async-start(bf16[64,2,108]{2,1,0:T(2,128)(2,1)} %bitcast.7), calls=%async_computation.2 | async-start | bytes 65536 | tf_op jit(solution)/shard_map/all_to_all | solution.py:105
  79.1 39.6 %all-to-all-start.3 = ((bf16[64,288,18]{1,2,0:T(8,128)(2,1)}), bf16[64,288,18]{1,2,0:T(8,128)(2,1)}, u32[]{:S(2)}, u32[]{:S(2)}) async-start(bf16[64,288,18]{1,2,0:T(8,128)(2,1)} %broadcast_in_dim.85), calls=%async_computation.3 | async-start | bytes 2359296 | tf_op jit(solution)/shard_map/all_to_all | solution.py:20
  85.5 196.3 %all-gather.16.cloned.1.call-start = ((), (), s32[]{:S(2)}) async-start(), calls=%async_computation.9 | async-start | bytes 5898240 | tf_op jit(solution)/shard_map/all_gather | solution.py:14
  187.2 2.4 copy-start.3
  187.6 24.7 %copy-start.4 = (bf16[1152,18]{0,1:T(8,128)(2,1)S(1)}, bf16[1152,18]{0,1:T(8,128)(2,1)}, u32[]{:S(2)}) copy-start(bf16[1152,18]{0,1:T(8,128)(2,1)} %param.26) | copy-start | bytes 124420
  189.5 46.7 %copy-start.7 = (bf16[2,288]{1,0:T(2,128)(2,1)S(1)}, bf16[2,288]{1,0:T(2,128)(2,1)}, u32[]{:S(2)}) copy-start(bf16[2,288]{1,0:T(2,128)(2,1)} %copy-done.6) | copy-start | bytes 3460
  189.5 139.1 %all-gather.12.cloned.1.call-start = ((), (), s32[]{:S(2)}) async-start(), calls=%async_computation.7 | async-start | bytes 2985984 | tf_op jit(solution)/shard_map/all_gather | solution.py:41
  212.3 162.0 %all-gather.14.cloned.1.call-start = ((), (), s32[]{:S(2)}) async-start(), calls=%async_computation.8 | async-start | bytes 2985984 | tf_op jit(solution)/shard_map/all_gather | solution.py:41
  237.2 141.8 %all-to-all-start.5 = ((bf16[4,2,2304]{2,1,0:T(2,128)(2,1)}), bf16[4,2,2304]{2,1,0:T(2,128)(2,1)S(1)}, u32[]{:S(2)}, u32[]{:S(2)}) async-start(bf16[4,2,2304]{2,1,0:T(2,128)(2,1)} %broadcast_in_dim.86), calls=%async_computation.5 | async-start | bytes 73728 | tf_op jit(solution)/shard_map/all_to_all | solution.py:20
  287.9 1.4 copy-start.1
  287.9 2.1 copy-start.2
  379.0 30.5 %all-to-all-start.4 = ((bf16[4,64,2,1152]{3,1,2,0:T(8,128)(2,1)}), bf16[4,64,2,1152]{3,1,2,0:T(8,128)(2,1)S(1)}, u32[]{:S(2)}, u32[]{:S(2)}) async-start(bf16[4,64,2,1152]{3,1,2,0:T(8,128)(2,1)} %copy.113), calls=%async_computation.4 | async-start | bytes 2359296 | tf_op jit(solution)/shard_map/all_to_all | solution.py:53
  384.0 27.1 %copy-start.8 = (bf16[1152,16]{0,1:T(8,128)(2,1)S(1)}, bf16[1152,16]{0,1:T(8,128)(2,1)}, u32[]{:S(2)}) copy-start(bf16[1152,16]{0,1:T(8,128)(2,1)} %param.27) | copy-start | bytes 110596
Sparse Core Ops, SparseCore 0:
  11.7 160.3 all-gather.9
  189.7 92.1 all-gather.15
  283.9 44.6 all-gather.11
  330.5 43.6 all-gather.13
